TPU v7x, 32 devices: a whole 2x2x4 slice. The times are simulated.
32 devices in a mesh: seq: 4 (over y, x), fsdp: 8 (over z, core).
Axes of the slice: x: 2, y: 2, z: 4, core: 2. Of those that a mesh axis runs over, the one named last changes fastest.
Arguments:
- hidden_in: bfloat16 [8, 1024, 2048], P('fsdp', 'seq'), may hold values from -6 to 6
- cotangent: bfloat16 [8, 1024, 2048], P('fsdp', 'seq'), may hold values from -6 to 6
- block_table: int32 [4, 2], replicated, may hold values from 0 to 7, as said below
- first_gain: bfloat16 [2048], P('fsdp'), may hold values from 0.5 to 1.5
- first_bias: bfloat16 [2048], P('fsdp'), may hold values from -3 to 3
- qkv_weight: bfloat16 [2048, 6144], P('fsdp'), may hold values from -0.125 to 0.125
- qkv_bias: bfloat16 [6144], P('fsdp')
- out_weight: bfloat16 [2048, 2048], P('fsdp'), may hold values from -2 to 2
- second_gain: bfloat16 [2048], P('fsdp'), may hold values from 0.5 to 1.5
- second_bias: bfloat16 [2048], P('fsdp'), may hold values from -3 to 3
- gate_weight: bfloat16 [2048, 5632], P('fsdp'), may hold values from -0.125 to 0.125
- up_weight: bfloat16 [2048, 5632], P('fsdp'), may hold values from -0.125 to 0.125
- down_weight: bfloat16 [5632, 2048], P('fsdp'), may hold values from -0.078125 to 0.078125
Outputs:
- block_out: bfloat16 [8, 1024, 2048], P('fsdp', 'seq')
- input_grad: bfloat16 [8, 1024, 2048], P('fsdp', 'seq')
- first_gain_grad: float32 [2048], P('fsdp')
- first_bias_grad: float32 [2048], P('fsdp')
- qkv_weight_grad: float32 [2048, 6144], P('fsdp')
- qkv_bias_grad: float32 [6144], P('fsdp')
- out_weight_grad: float32 [2048, 2048], P('fsdp')
- second_gain_grad: float32 [2048], P('fsdp')
- second_bias_grad: float32 [2048], P('fsdp')
- gate_weight_grad: float32 [2048, 5632], P('fsdp')
- up_weight_grad: float32 [2048, 5632], P('fsdp')
- down_weight_grad: float32 [5632, 2048], P('fsdp')
Inputs may be any that keep to these rules, and one draw needn't show every extreme that they name: `block_table`: row i holds a pair b and 7 - b, in either order; every block number appears once in the table; the same table holds for all sequences.
All inputs are finite; a program needn't handle non-finite values.
Results may differ from a plain program's by a relative error of at most 0.028.
The roundings to bfloat16 on the way count: a program that leaves them out, or rounds other values in their place, can miss the bound.
Values may be sent and summed in bfloat16 or wider, within the bound.
A program may use at most 448 MiB of HBM per device.

v0:
```python
import jax
import jax.numpy as jnp
from jax import lax
from jax.sharding import PartitionSpec as P

HEADS = 32
HD = 64
EPS = 1e-05
ROPE_BASE = 10000.0
NEG = -1e30


def normalize(values):
    centred = values - jnp.mean(values, axis=-1, keepdims=True)
    inverse = lax.rsqrt(jnp.mean(centred * centred, axis=-1, keepdims=True) + EPS)
    return (centred * inverse, inverse)


def norm_back(d_normed, centred_scaled, inverse, gain):
    scaled = d_normed * gain
    return inverse * (
        scaled
        - jnp.mean(scaled, axis=-1, keepdims=True)
        - centred_scaled * jnp.mean(scaled * centred_scaled, axis=-1, keepdims=True)
    )


def rotate(tensor, places, direction):
    head_dim = tensor.shape[-1]
    rotated = head_dim // 4
    half = rotated // 2
    freq = ROPE_BASE ** (-(jnp.arange(half, dtype=jnp.float32) * 2.0) / rotated)
    angle = places.astype(jnp.float32)[:, None] * freq[None, :]
    cosine = jnp.cos(angle)[:, None, :]
    sine = direction * jnp.sin(angle)[:, None, :]
    first = tensor[..., :half]
    second = tensor[..., half:rotated]
    return jnp.concatenate(
        [first * cosine - second * sine, second * cosine + first * sine, tensor[..., rotated:]],
        axis=-1,
    )


def body(
    hidden_in,
    cotangent,
    block_table,
    first_gain,
    first_bias,
    qkv_weight,
    qkv_bias,
    out_weight,
    second_gain,
    second_bias,
    gate_weight,
    up_weight,
    down_weight,
):
    inputs = hidden_in[0].astype(jnp.float32)
    tokens = inputs.shape[0]
    width = inputs.shape[1]
    half_rows = tokens // 2
    heads = HEADS
    head_dim = HD
    group = min(8, heads)
    groups = heads // group
    scale = float(head_dim) ** (-0.5)
    ffn_width = gate_weight.shape[1]
    own_pair = lax.dynamic_slice_in_dim(block_table, lax.axis_index("seq"), 1, 0)[0]
    offsets = jnp.arange(half_rows, dtype=jnp.int32)
    places = (own_pair[:, None] * half_rows + offsets[None, :]).reshape(tokens)
    key_places = (block_table[:, :, None] * half_rows + offsets[None, None, :]).reshape(-1)
    visible = key_places[None, :] <= places[:, None]
    gain_one, bias_one, w_qkv_full, b_qkv_full, w_out_full = (
        lax.all_gather(first_gain, "fsdp", axis=0, tiled=True),
        lax.all_gather(first_bias, "fsdp", axis=0, tiled=True),
        lax.all_gather(qkv_weight, "fsdp", axis=0, tiled=True),
        lax.all_gather(qkv_bias, "fsdp", axis=0, tiled=True),
        lax.all_gather(out_weight, "fsdp", axis=0, tiled=True),
    )
    centred_one, inverse_one = normalize(inputs)
    normed_one = (centred_one * gain_one.astype(jnp.float32) + bias_one.astype(jnp.float32)).astype(
        jnp.bfloat16
    )
    projected = jnp.dot(
        normed_one, w_qkv_full, preferred_element_type=jnp.float32
    ) + b_qkv_full.astype(jnp.float32)
    query = rotate(projected[:, :width].reshape(tokens, heads, head_dim), places, 1.0).astype(
        jnp.bfloat16
    )
    key_rot = rotate(
        projected[:, width : 2 * width].reshape(tokens, heads, head_dim), places, 1.0
    ).astype(jnp.bfloat16)
    value_own = projected[:, 2 * width :].astype(jnp.bfloat16)
    key_all, value_all = (
        lax.all_gather(key_rot.reshape(tokens, width), "seq", axis=0, tiled=True),
        lax.all_gather(value_own, "seq", axis=0, tiled=True),
    )
    key_heads = key_all.reshape(-1, heads, head_dim)
    value_heads = value_all.reshape(-1, heads, head_dim)

    def group_scores(index):
        query_group = lax.dynamic_slice_in_dim(query, index * group, group, 1)
        key_group = lax.dynamic_slice_in_dim(key_heads, index * group, group, 1)
        value_group = lax.dynamic_slice_in_dim(value_heads, index * group, group, 1)
        scores = (
            jnp.einsum("qgd,kgd->gqk", query_group, key_group, preferred_element_type=jnp.float32)
            * scale
        )
        scores = jnp.where(visible[None], scores, NEG)
        return (query_group, key_group, value_group, scores)

    def forward_group(index):
        query_group, key_group, value_group, scores = group_scores(index)
        peak = jnp.max(scores, axis=-1, keepdims=True)
        log_total = peak + jnp.log(jnp.sum(jnp.exp(scores - peak), axis=-1, keepdims=True))
        weights = jnp.exp(scores - log_total).astype(jnp.bfloat16)
        return (
            jnp.einsum("gqk,kgd->qgd", weights, value_group, preferred_element_type=jnp.float32),
            log_total,
        )

    head_out, log_totals = lax.map(forward_group, jnp.arange(groups))
    mixed = head_out.transpose(1, 0, 2, 3).reshape(tokens, width).astype(jnp.bfloat16)
    residual = inputs + jnp.dot(mixed, w_out_full, preferred_element_type=jnp.float32)
    gain_two, bias_two, w_gate_full, w_up_full, w_down_full = (
        lax.all_gather(second_gain, "fsdp", axis=0, tiled=True),
        lax.all_gather(second_bias, "fsdp", axis=0, tiled=True),
        lax.all_gather(gate_weight, "fsdp", axis=0, tiled=True),
        lax.all_gather(up_weight, "fsdp", axis=0, tiled=True),
        lax.all_gather(down_weight, "fsdp", axis=0, tiled=True),
    )
    centred_two, inverse_two = normalize(residual)
    normed_two = (centred_two * gain_two.astype(jnp.float32) + bias_two.astype(jnp.float32)).astype(
        jnp.bfloat16
    )
    gate = jnp.dot(normed_two, w_gate_full, preferred_element_type=jnp.float32)
    upward = jnp.dot(normed_two, w_up_full, preferred_element_type=jnp.float32)
    sigmoid = jax.nn.sigmoid(gate)
    activated = (gate * sigmoid * upward).astype(jnp.bfloat16)
    block_out = (
        residual + jnp.dot(activated, w_down_full, preferred_element_type=jnp.float32)
    ).astype(jnp.bfloat16)
    gain_one, w_qkv_full, w_out_full = (
        lax.all_gather(first_gain, "fsdp", axis=0, tiled=True),
        lax.all_gather(qkv_weight, "fsdp", axis=0, tiled=True),
        lax.all_gather(out_weight, "fsdp", axis=0, tiled=True),
    )
    gain_two, w_gate_full, w_up_full, w_down_full = (
        lax.all_gather(second_gain, "fsdp", axis=0, tiled=True),
        lax.all_gather(gate_weight, "fsdp", axis=0, tiled=True),
        lax.all_gather(up_weight, "fsdp", axis=0, tiled=True),
        lax.all_gather(down_weight, "fsdp", axis=0, tiled=True),
    )
    d_out = cotangent[0].astype(jnp.float32)
    d_branch = d_out.astype(jnp.bfloat16)
    d_activated = jnp.einsum("rd,fd->rf", d_branch, w_down_full, preferred_element_type=jnp.float32)
    d_gate = (d_activated * upward * sigmoid * (1.0 + gate * (1.0 - sigmoid))).astype(jnp.bfloat16)
    d_upward = (d_activated * gate * sigmoid).astype(jnp.bfloat16)
    d_normed_two = jnp.einsum(
        "rf,df->rd", d_gate, w_gate_full, preferred_element_type=jnp.float32
    ) + jnp.einsum("rf,df->rd", d_upward, w_up_full, preferred_element_type=jnp.float32)
    gain_two_grad = jnp.sum(d_normed_two * centred_two, axis=0)
    bias_two_grad = jnp.sum(d_normed_two, axis=0)
    d_residual = d_out + norm_back(
        d_normed_two, centred_two, inverse_two, gain_two.astype(jnp.float32)
    )
    gate_up_rows = jnp.concatenate([d_gate, d_upward], axis=1)
    d_attended = d_residual.astype(jnp.bfloat16)
    normed_slice = normed_two
    gate_up_grad = lax.psum_scatter(
        jnp.einsum(
            "rd,rf->df", normed_slice, gate_up_rows, preferred_element_type=jnp.float32
        ).astype(jnp.bfloat16),
        "fsdp",
        scatter_dimension=0,
        tiled=True,
    )
    down_grad = lax.psum_scatter(
        jnp.einsum("rf,rd->fd", activated, d_branch, preferred_element_type=jnp.float32).astype(
            jnp.bfloat16
        ),
        "fsdp",
        scatter_dimension=0,
        tiled=True,
    )
    out_grad = lax.psum_scatter(
        jnp.einsum("rd,re->de", mixed, d_attended, preferred_element_type=jnp.float32).astype(
            jnp.bfloat16
        ),
        "fsdp",
        scatter_dimension=0,
        tiled=True,
    )
    d_mixed = (
        jnp.einsum("re,de->rd", d_attended, w_out_full, preferred_element_type=jnp.float32)
        .astype(jnp.bfloat16)
        .reshape(tokens, heads, head_dim)
    )

    def backward_group(packed):
        index, log_total = packed
        query_group, key_group, value_group, scores = group_scores(index)
        probs = jnp.exp(scores - log_total)
        d_group = lax.dynamic_slice_in_dim(d_mixed, index * group, group, 1)
        d_probs = jnp.einsum(
            "qgd,kgd->gqk", d_group, value_group, preferred_element_type=jnp.float32
        )
        d_scores = (probs * (d_probs - jnp.sum(d_probs * probs, axis=-1, keepdims=True))).astype(
            jnp.bfloat16
        )
        d_query = (
            jnp.einsum("gqk,kgd->qgd", d_scores, key_group, preferred_element_type=jnp.float32)
            * scale
        )
        d_key = (
            jnp.einsum("gqk,qgd->kgd", d_scores, query_group, preferred_element_type=jnp.float32)
            * scale
        )
        d_value = jnp.einsum(
            "gqk,qgd->kgd", probs.astype(jnp.bfloat16), d_group, preferred_element_type=jnp.float32
        )
        return (d_query, d_key, d_value)

    d_query_all, d_key_all, d_value_all = lax.map(backward_group, (jnp.arange(groups), log_totals))
    d_query = d_query_all.transpose(1, 0, 2, 3).reshape(tokens, heads, head_dim)
    d_key_full = d_key_all.transpose(1, 0, 2, 3).reshape(-1, width)
    d_value_full = d_value_all.transpose(1, 0, 2, 3).reshape(-1, width)
    d_key_own, d_value_own = (
        lax.psum_scatter(d_key_full, "seq", scatter_dimension=0, tiled=True),
        lax.psum_scatter(d_value_full, "seq", scatter_dimension=0, tiled=True),
    )
    d_projected = jnp.concatenate(
        [
            rotate(d_query, places, -1.0).reshape(tokens, width),
            rotate(d_key_own.reshape(tokens, heads, head_dim), places, -1.0).reshape(tokens, width),
            d_value_own,
        ],
        axis=1,
    ).astype(jnp.bfloat16)
    qkv_bias_term = jnp.sum(d_projected.astype(jnp.float32), axis=0)
    d_normed_one = jnp.einsum(
        "re,de->rd", d_projected, w_qkv_full, preferred_element_type=jnp.float32
    )
    gain_one_grad = jnp.sum(d_normed_one * centred_one, axis=0)
    bias_one_grad = jnp.sum(d_normed_one, axis=0)
    input_grad = (
        d_residual + norm_back(d_normed_one, centred_one, inverse_one, gain_one.astype(jnp.float32))
    ).astype(jnp.bfloat16)
    normed_slice = normed_one
    qkv_grad = lax.psum_scatter(
        jnp.einsum(
            "rd,re->de", normed_slice, d_projected, preferred_element_type=jnp.float32
        ).astype(jnp.bfloat16),
        "fsdp",
        scatter_dimension=0,
        tiled=True,
    )
    gain_one_part, bias_one_part, qkv_bias_part, gain_two_part, bias_two_part = (
        lax.psum_scatter(
            gain_one_grad.astype(jnp.bfloat16), "fsdp", scatter_dimension=0, tiled=True
        ).astype(jnp.float32),
        lax.psum_scatter(
            bias_one_grad.astype(jnp.bfloat16), "fsdp", scatter_dimension=0, tiled=True
        ).astype(jnp.float32),
        lax.psum_scatter(
            qkv_bias_term.astype(jnp.bfloat16), "fsdp", scatter_dimension=0, tiled=True
        ).astype(jnp.float32),
        lax.psum_scatter(
            gain_two_grad.astype(jnp.bfloat16), "fsdp", scatter_dimension=0, tiled=True
        ).astype(jnp.float32),
        lax.psum_scatter(
            bias_two_grad.astype(jnp.bfloat16), "fsdp", scatter_dimension=0, tiled=True
        ).astype(jnp.float32),
    )
    summed = (
        lax.psum(gain_one_part.astype(jnp.bfloat16), "seq").astype(jnp.float32),
        lax.psum(bias_one_part.astype(jnp.bfloat16), "seq").astype(jnp.float32),
        lax.psum(qkv_grad, "seq").astype(jnp.float32),
        lax.psum(qkv_bias_part.astype(jnp.bfloat16), "seq").astype(jnp.float32),
        lax.psum(out_grad, "seq").astype(jnp.float32),
        lax.psum(gain_two_part.astype(jnp.bfloat16), "seq").astype(jnp.float32),
        lax.psum(bias_two_part.astype(jnp.bfloat16), "seq").astype(jnp.float32),
        lax.psum(gate_up_grad, "seq").astype(jnp.float32),
        lax.psum(down_grad, "seq").astype(jnp.float32),
    )
    gate_up_total = summed[7]
    return (
        block_out[None],
        input_grad[None],
        summed[0],
        summed[1],
        summed[2],
        summed[3],
        summed[4],
        summed[5],
        summed[6],
        gate_up_total[:, :ffn_width],
        gate_up_total[:, ffn_width:],
        summed[8],
    )


def solution(mesh):
    return jax.shard_map(
        body,
        mesh=mesh,
        in_specs=(
            P("fsdp", "seq", None),
            P("fsdp", "seq", None),
            P(),
            P("fsdp"),
            P("fsdp"),
            P("fsdp", None),
            P("fsdp"),
            P("fsdp", None),
            P("fsdp"),
            P("fsdp"),
            P("fsdp", None),
            P("fsdp", None),
            P("fsdp", None),
        ),
        out_specs=(
            P("fsdp", "seq", None),
            P("fsdp", "seq", None),
            P("fsdp"),
            P("fsdp"),
            P("fsdp", None),
            P("fsdp"),
            P("fsdp", None),
            P("fsdp"),
            P("fsdp"),
            P("fsdp", None),
            P("fsdp", None),
            P("fsdp", None),
        ),
        check_vma=False,
    )
```

profile of v0, /device:TPU:0, one launch (start us, length us, event | category | flops | bytes accessed | tf_op | source)
XLA Modules:
  0.0 2643.6 jit_solution(6911663697845199274)
XLA Ops:
  8.0 15.7 all-gather.2
  48.4 184.0 %all-gather.13.cloned.1.call-done = bf16[2048,6144]{1,0:T(8,128)(2,1)} async-done(((bf16[256,6144]{1,0:T(8,128)(2,1)}), bf16[2048,6144]{1,0:T(8,128)(2,1)}) %all-gather.13.cloned.1.call-update) | async-done | bytes 25165840 | tf_op jit(solution)/shard_map/all_gather | solution.py:77
  305.5 48.3 %all-gather.17.cloned.1.call-done = bf16[1024,2048]{0,1:T(8,128)(2,1)} async-done(((bf16[256,2048]{0,1:T(8,128)(2,1)}), bf16[1024,2048]{0,1:T(8,128)(2,1)}) %all-gather.17.cloned.1.call-update) | async-done | bytes 4194320 | tf_op jit(solution)/shard_map/all_gather | solution.py:96
  353.8 39.9 %while.30 = (s32[]{:T(128)}, bf16[4,256,8,64]{1,3,2,0:T(8,128)(2,1)S(1)}, f32[4,8,256,1]{2,1,3,0:T(8,128)S(1)}, s32[4]{0:T(128)S(1)}, bf16[1024,32,64]{0,2,1:T(8...) while((s32[]{:T(128)}, ...), condition=%wide.region_5.6_spmd.clone.clone, body=%wide.region_2.5_spmd.clone.sunk.clone | while | flops 560199680 | bytes 29169844 | solution.py:123
  393.8 43.6 %all-gather.19.cloned.1.call-done = bf16[2048,2048]{1,0:T(8,128)(2,1)} async-done(((bf16[256,2048]{1,0:T(8,128)(2,1)}), bf16[2048,2048]{1,0:T(8,128)(2,1)}) %all-gather.19.cloned.1.call-update) | async-done | bytes 8388624 | tf_op jit(solution)/shard_map/all_gather | solution.py:79
  443.9 196.1 %all-gather.21.cloned.1.call-done = bf16[2048,5632]{1,0:T(8,128)(2,1)} async-done(((bf16[256,5632]{1,0:T(8,128)(2,1)}), bf16[2048,5632]{1,0:T(8,128)(2,1)}) %all-gather.21.cloned.1.call-update) | async-done | bytes 23068688 | tf_op jit(solution)/shard_map/all_gather | solution.py:129
  640.0 15.1 fusion.79
  655.1 187.3 %all-gather.23.cloned.1.call-done = bf16[2048,5632]{1,0:T(8,128)(2,1)} async-done(((bf16[256,5632]{1,0:T(8,128)(2,1)}), bf16[2048,5632]{1,0:T(8,128)(2,1)}) %all-gather.23.cloned.1.call-update) | async-done | bytes 23068688 | tf_op jit(solution)/shard_map/all_gather | solution.py:130
  842.4 14.9 fusion.78
  857.3 187.6 %all-gather.25.cloned.1.call-done = bf16[5632,2048]{1,0:T(8,128)(2,1)} async-done(((bf16[704,2048]{1,0:T(8,128)(2,1)}), bf16[5632,2048]{1,0:T(8,128)(2,1)}) %all-gather.25.cloned.1.call-update) | async-done | bytes 23068688 | tf_op jit(solution)/shard_map/all_gather | solution.py:131
  1044.9 26.2 multiply_convert_fusion.1
  1083.5 13.9 multiply_reduce_fusion.1
  1107.7 80.1 %while.31 = (s32[]{:T(128)}, f32[4,256,8,64]{1,3,2,0:T(8,128)}, f32[4,1024,8,64]{1,3,2,0:T(8,128)}, f32[4,1024,8,64]{1,3,2,0:T(8,128)}, s32[4]{0:T(128)S(1)}, /*...) while((s32[]{:T(128)}, f32[4,256,8,64]{1,3,2,0:T(8,128)}, ...), condition=%wide.region_12.13_spmd.clone.clone, body=%wide.region_10.12_spmd.clone.sunk.clone | while | flops 1374550016 | bytes 72940760 | solution.py:225
  1211.5 60.9 %reduce-scatter.9.cloned.1.call-done = f32[256,2048]{0,1:T(8,128)} async-done(((f32[1024,2048]{0,1:T(8,128)}), f32[256,2048]{0,1:T(8,128)}) %reduce-scatter.9.cloned.1.call-update) | async-done | bytes 2097168 | tf_op jit(solution)/shard_map/reduce_scatter | solution.py:230
  1274.0 87.9 %reduce-scatter.11.cloned.1.call-done = f32[256,2048]{0,1:T(8,128)} async-done(((f32[1024,2048]{0,1:T(8,128)}), f32[256,2048]{0,1:T(8,128)}) %reduce-scatter.11.cloned.1.call-update) | async-done | bytes 2097168 | tf_op jit(solution)/shard_map/reduce_scatter | solution.py:231
  1366.9 15.0 convolution_convert_fusion.2
  1383.6 21.3 convolution_convert_fusion
  1404.9 48.7 %reduce-scatter.15.cloned.1.call-done = bf16[256,2048]{1,0:T(8,128)(2,1)} async-done(((bf16[2048,2048]{1,0:T(8,128)(2,1)}), bf16[256,2048]{1,0:T(8,128)(2,1)}) %reduce-scatter.15.cloned.1.call-update) | async-done | bytes 1048592 | tf_op jit(solution)/shard_map/reduce_scatter | solution.py:187
  1453.6 228.2 %reduce-scatter.17.cloned.1.call-done = bf16[704,2048]{1,0:T(8,128)(2,1)} async-done(((bf16[5632,2048]{1,0:T(8,128)(2,1)}), bf16[704,2048]{1,0:T(8,128)(2,1)}) %reduce-scatter.17.cloned.1.call-update) | async-done | bytes 2883600 | tf_op jit(solution)/shard_map/reduce_scatter | solution.py:179
  1681.8 247.8 %reduce-scatter.13.cloned.1.call-done = bf16[256,6144]{1,0:T(8,128)(2,1)} async-done(((bf16[2048,6144]{1,0:T(8,128)(2,1)}), bf16[256,6144]{1,0:T(8,128)(2,1)}) %reduce-scatter.13.cloned.1.call-update) | async-done | bytes 3145744 | tf_op jit(solution)/shard_map/reduce_scatter | solution.py:251
  1929.6 444.5 %reduce-scatter.19.cloned.1.call-done = bf16[256,11264]{1,0:T(8,128)(2,1)} async-done(((bf16[2048,11264]{1,0:T(8,128)(2,1)}), bf16[256,11264]{1,0:T(8,128)(2,1)}) %reduce-scatter.19.cloned.1.call-update) | async-done | bytes 5767184
  2391.5 14.0 fusion.61
  2405.5 26.0 all-reduce.6
  2448.8 171.4 %all-reduce.11.cloned.1.call-done = (bf16[256,6144]{1,0:T(8,128)(2,1)}, bf16[256,2048]{1,0:T(8,128)(2,1)}, bf16[256,11264]{1,0:T(8,128)(2,1)}, bf16[704,2048]{1,0:T(8,128)(2,1)}) async-done(((bf16[256,6144]{1,0:T(8,128)(2,1)}, bf16[256,2048]{1,0:T(8,128)(2,1)}, bf16[256,11264]{1,0:T(8,128)(2,1)}, bf16[704,2048]{1,0:T(8,128)(2,1)}), (bf16[256,6144]{1,0:T(8,128)(2,1)}, bf16[256,2048]{1,0:T(8,128)(2,1)}, ...) | async-done | bytes 12845072 | tf_op jit(solution)/shard_map/psum | solution.py:279
  (275 shorter events, 323.0 us)
Async XLA Ops:
  7.2 225.2 %all-gather.13.cloned.1.call-start = ((), (), s32[]{:S(2)}) async-start(), calls=%async_computation.6 | async-start | bytes 28311552 | tf_op jit(solution)/shard_map/all_gather | solution.py:77
  8.0 291.0 %all-gather.15.cloned.1.call-start = ((), (), s32[]{:S(2)}) async-start(), calls=%async_computation.7 | async-start | bytes 5242880 | tf_op jit(solution)/shard_map/all_gather | solution.py:97
  35.9 208.3 %copy-start.26 = (f32[8,1,256]{2,1,0:T(1,128)}, f32[8,1,256]{2,1,0:T(1,128)S(1)}, u32[]{:S(2)}) copy-start(f32[8,1,256]{2,1,0:T(1,128)S(1)} %convert_element_type.193) | copy-start | bytes 24580
  47.7 196.5 %copy-start.22 = (f32[8,1,256]{2,1,0:T(1,128)}, f32[8,1,256]{2,1,0:T(1,128)S(1)}, u32[]{:S(2)}) copy-start(f32[8,1,256]{2,1,0:T(1,128)S(1)} %convert_element_type.192) | copy-start | bytes 24580
  47.9 196.3 %copy-start.34 = (f32[256]{0:T(256)}, f32[256]{0:T(256)S(1)}, u32[]{:S(2)}) copy-start(f32[256]{0:T(256)S(1)} %broadcast_multiply_fusion.7) | copy-start | bytes 3076
  48.4 195.8 %copy-start.36 = (f32[256]{0:T(256)}, f32[256]{0:T(256)S(1)}, u32[]{:S(2)}) copy-start(f32[256]{0:T(256)S(1)} %add_rsqrt_fusion.1) | copy-start | bytes 3076
  248.1 105.7 %all-gather.17.cloned.1.call-start = ((), (), s32[]{:S(2)}) async-start(), calls=%async_computation.8 | async-start | bytes 5242880 | tf_op jit(solution)/shard_map/all_gather | solution.py:96
  261.9 175.4 %all-gather.19.cloned.1.call-start = ((), (), s32[]{:S(2)}) async-start(), calls=%async_computation.9 | async-start | bytes 9437184 | tf_op jit(solution)/shard_map/all_gather | solution.py:79
  262.5 377.5 %all-gather.21.cloned.1.call-start = ((), (), s32[]{:S(2)}) async-start(), calls=%async_computation.10 | async-start | bytes 25952256 | tf_op jit(solution)/shard_map/all_gather | solution.py:129
  263.1 579.2 %all-gather.23.cloned.1.call-start = ((), (), s32[]{:S(2)}) async-start(), calls=%async_computation.11 | async-start | bytes 25952256 | tf_op jit(solution)/shard_map/all_gather | solution.py:130
  263.7 781.2 %all-gather.25.cloned.1.call-start = ((), (), s32[]{:S(2)}) async-start(), calls=%async_computation.12 | async-start | bytes 25952256 | tf_op jit(solution)/shard_map/all_gather | solution.py:131
  264.5 1008.0 %reduce-scatter.9.cloned.1.call-start = ((), (), s32[]{:S(2)}) async-start(), calls=%async_computation.13 | async-start | bytes 10485760 | tf_op jit(solution)/shard_map/reduce_scatter | solution.py:230
  273.3 569.0 %copy-start.28 = (f32[8,1,256]{2,1,0:T(1,128)}, f32[8,1,256]{2,1,0:T(1,128)S(1)}, u32[]{:S(2)}) copy-start(f32[8,1,256]{2,1,0:T(1,128)S(1)} %convert_element_type.196) | copy-start | bytes 24580
  283.5 813.9 %copy-start.24 = (f32[8,1,256]{2,1,0:T(1,128)}, f32[8,1,256]{2,1,0:T(1,128)S(1)}, u32[]{:S(2)}) copy-start(f32[8,1,256]{2,1,0:T(1,128)S(1)} %convert_element_type.195) | copy-start | bytes 24580
  443.5 654.0 %copy-start = (f32[256,2048]{1,0:T(8,128)}, f32[256,2048]{1,0:T(8,128)S(1)}, u32[]{:S(2)}) copy-start(f32[256,2048]{1,0:T(8,128)S(1)} %get-tuple-element.285) | copy-start | bytes 6291460
  443.5 653.9 %copy-start.30 = (f32[256]{0:T(256)}, f32[256]{0:T(256)S(1)}, u32[]{:S(2)}) copy-start(f32[256]{0:T(256)S(1)} %broadcast_multiply_fusion.6) | copy-start | bytes 3076
  443.9 653.6 %copy-start.32 = (f32[256]{0:T(256)}, f32[256]{0:T(256)S(1)}, u32[]{:S(2)}) copy-start(f32[256]{0:T(256)S(1)} %add_rsqrt_fusion) | copy-start | bytes 3076
  655.1 389.8 %copy-start.19 = (bf16[1,256,2048]{2,1,0:T(8,128)(2,1)S(1)}, bf16[1,256,2048]{2,1,0:T(8,128)(2,1)}, u32[]{:S(2)}) copy-start(bf16[1,256,2048]{2,1,0:T(8,128)(2,1)} %param.18) | copy-start | bytes 3145732
  1187.8 174.1 %reduce-scatter.11.cloned.1.call-start = ((), (), s32[]{:S(2)}) async-start(), calls=%async_computation.14 | async-start | bytes 10485760 | tf_op jit(solution)/shard_map/reduce_scatter | solution.py:231
  1188.5 265.0 %reduce-scatter.15.cloned.1.call-start = ((), (), s32[]{:S(2)}) async-start(), calls=%async_computation.16 | async-start | bytes 9437184 | tf_op jit(solution)/shard_map/reduce_scatter | solution.py:187
  1195.4 486.4 %reduce-scatter.17.cloned.1.call-start = ((), (), s32[]{:S(2)}) async-start(), calls=%async_computation.17 | async-start | bytes 25952256 | tf_op jit(solution)/shard_map/reduce_scatter | solution.py:179
  1209.7 719.8 %reduce-scatter.13.cloned.1.call-start = ((), (), s32[]{:S(2)}) async-start(), calls=%async_computation.15 | async-start | bytes 28311552 | tf_op jit(solution)/shard_map/reduce_scatter | solution.py:251
  1382.0 992.1 %reduce-scatter.19.cloned.1.call-start = ((), (), s32[]{:S(2)}) async-start(), calls=%async_computation.18 | async-start | bytes 51904512
  1404.9 1215.4 %all-reduce.11.cloned.1.call-start = ((), (), s32[]{:S(2)}) async-start(), calls=%async_computation.19 | async-start | bytes 25690112 | tf_op jit(solution)/shard_map/psum | solution.py:279
  (42 other events, 698.5 us)
Sparse Core Ops, SparseCore 0:
  9.7 222.6 all-gather.12
  248.2 50.6 all-gather.14
  301.3 52.4 all-gather.16
  355.3 82.0 all-gather.18
  438.8 201.1 all-gather.20
  641.5 200.8 all-gather.22
  844.0 200.8 all-gather.24
  1187.9 84.4 reduce-scatter.8
  1275.5 86.3 reduce-scatter.10
  1364.0 89.5 reduce-scatter.14
  1456.0 225.7 reduce-scatter.16
  1684.0 245.5 reduce-scatter.12
  1932.0 442.1 reduce-scatter.18
  2377.9 242.2 all-reduce.10
where the time goes:
time: 2650 us; the launch traced here: 2640 us
  waiting for transfers between devices  2150 us (81%)
  matrix products  278 us (10%)
  blocking collectives  94.9 us (4%)
  other arithmetic  48.4 us (2%)
  local copies, waits for them, and re-layouts  45.4 us (2%)
    unnamed x15, waiting for transfers between devices  448 us
    reduce_scatter x1, waiting for transfers between devices, body(): lax.psum_scatter(jnp.einsum('rd,re->de', normed_slice, d_projected, prefe...  248 us
    reduce_scatter x1, waiting for transfers between devices, body(): lax.psum_scatter(jnp.einsum('rf,rd->fd', activated, d_branch, preferred_e...  228 us
    all_gather x1, waiting for transfers between devices, body(): lax.all_gather(gate_weight, 'fsdp', axis=0, tiled=True)  196 us
    all_gather x1, waiting for transfers between devices, body(): lax.all_gather(down_weight, 'fsdp', axis=0, tiled=True)  188 us
    all_gather x1, waiting for transfers between devices, body(): lax.all_gather(up_weight, 'fsdp', axis=0, tiled=True)  187 us
    all_gather x1, waiting for transfers between devices, body(): lax.all_gather(qkv_weight, 'fsdp', axis=0, tiled=True)  184 us
    psum x1, waiting for transfers between devices, body(): lax.psum(qkv_grad, 'seq').astype(jnp.float32)  171 us
  transfers between devices with their start and end apart: 14, of which 14 were waited for; matrix products, arithmetic and copies ran while one was open for 7% of the time, Pallas kernels for 0%

commit v1 on v0

--- a/solution.py
+++ b/solution.py
@@ -1,3 +1,4 @@
+import functools
 import jax
 import jax.numpy as jnp
 from jax import lax
@@ -8,6 +9,15 @@
 EPS = 1e-05
 ROPE_BASE = 10000.0
 NEG = -1e30
+
+
+def _solve_panels(content, axis_id):
+    d_next = lax.all_to_all(jnp.stack(lax.axis_size(axis_id) * [content], axis=0), axis_id, 0, 0)
+    base_arr = jnp.concatenate(d_next, axis=0)
+    return base_arr
+
+
+connect_the_loads = functools.partial(_solve_panels, axis_id="fsdp")
 
 
 def normalize(values):
@@ -127,7 +137,7 @@
         lax.all_gather(second_gain, "fsdp", axis=0, tiled=True),
         lax.all_gather(second_bias, "fsdp", axis=0, tiled=True),
         lax.all_gather(gate_weight, "fsdp", axis=0, tiled=True),
-        lax.all_gather(up_weight, "fsdp", axis=0, tiled=True),
+        connect_the_loads(up_weight),
         lax.all_gather(down_weight, "fsdp", axis=0, tiled=True),
     )
     centred_two, inverse_two = normalize(residual)

time: 2650 us -> 2990 us (1.13)
  blocking collectives: 94.9 us -> 942 us
  waiting for transfers between devices: 2150 us -> 1630 us
    all_gather x1, blocking collectives: 8.65 us -> 597 us  [body(): lax.all_gather(second_bias, 'fsdp', axis=0, tiled=True)]
    all_gather x1, blocking collectives: 10.2 us -> 269 us  [body(): lax.all_gather(second_gain, 'fsdp', axis=0, tiled=True)]
    all_gather x1, waiting for transfers between devices: 196 us -> 0.01 us  [body(): lax.all_gather(gate_weight, 'fsdp', axis=0, tiled=True)]
    all_gather x1, waiting for transfers between devices: 188 us -> 0.01 us  [body(): lax.all_gather(down_weight, 'fsdp', axis=0, tiled=True)]
    all_gather x1, waiting for transfers between devices: 48.3 us -> 0.01 us  [body(): lax.all_gather(key_rot.reshape(tokens, width), 'seq', axis=0, tiled=True)]
    all_gather x1, waiting for transfers between devices: 43.6 us -> 0.02 us  [body(): lax.all_gather(out_weight, 'fsdp', axis=0, tiled=True)]
    all_gather x1, waiting for transfers between devices: 187 us -> 151 us  [body(): lax.all_gather(up_weight, 'fsdp', axis=0, tiled=True)]
  transfers between devices with their start and end apart: 14 -> 15, of which waited for: 14 -> 9; matrix products, arithmetic and copies ran while one was open for 7% -> 8% of each run, Pallas kernels for 0% -> 0%
where the time goes in v1:
time: 2990 us; the launch traced here: 2980 us
  waiting for transfers between devices  1630 us (55%)
  blocking collectives  942 us (32%)
  matrix products  278 us (9%)
  local copies, waits for them, and re-layouts  55.8 us (2%)
  other arithmetic  48.5 us (2%)
    all_gather x1, blocking collectives, body(): lax.all_gather(second_bias, 'fsdp', axis=0, tiled=True)  597 us
    unnamed x15, waiting for transfers between devices  448 us
    all_gather x1, blocking collectives, body(): lax.all_gather(second_gain, 'fsdp', axis=0, tiled=True)  269 us
    reduce_scatter x1, waiting for transfers between devices, body(): lax.psum_scatter(jnp.einsum('rd,re->de', normed_slice, d_projected, prefe...  248 us
    reduce_scatter x1, waiting for transfers between devices, body(): lax.psum_scatter(jnp.einsum('rf,rd->fd', activated, d_branch, preferred_e...  228 us
    all_gather x1, waiting for transfers between devices, body(): lax.all_gather(qkv_weight, 'fsdp', axis=0, tiled=True)  184 us
    psum x1, waiting for transfers between devices, body(): lax.psum(qkv_grad, 'seq').astype(jnp.float32)  171 us
    all_gather x1, waiting for transfers between devices, body(): lax.all_gather(up_weight, 'fsdp', axis=0, tiled=True)  151 us
  transfers between devices with their start and end apart: 15, of which 9 were waited for; matrix products, arithmetic and copies ran while one was open for 8% of the time, Pallas kernels for 0%

profile of v1, /device:TPU:0, one launch (start us, length us, event | category | flops | bytes accessed | tf_op | source)
XLA Modules:
  0.0 2981.7 jit_solution(960024673413253234)
XLA Ops:
  8.0 15.7 all-gather.2
  48.4 184.0 %all-gather.13.cloned.1.call-done = bf16[2048,6144]{1,0:T(8,128)(2,1)} async-done(((bf16[256,6144]{1,0:T(8,128)(2,1)}), bf16[2048,6144]{1,0:T(8,128)(2,1)}) %all-gather.13.cloned.1.call-update) | async-done | bytes 25165840 | tf_op jit(solution)/shard_map/all_gather | solution.py:87
  280.1 596.9 %all-gather.4 = bf16[8,1,256]{2,1,0:T(2,128)(2,1)S(1)} all-gather(bf16[1,1,256]{2,1,0:T(2,128)(2,1)S(1)} %reshape.295), channel_id=1, replica_groups=mesh['seq'=4,'fsdp'=8] {'fsdp'}, dimensions={0}, use_global_device_ids=true | all-gather | bytes 4608 | tf_op jit(solution)/shard_map/all_gather | solution.py:138
  877.1 268.7 %all-gather.3 = bf16[8,1,256]{2,1,0:T(2,128)(2,1)S(1)} all-gather(bf16[1,1,256]{2,1,0:T(2,128)(2,1)S(1)} %reshape.293), channel_id=1, replica_groups=mesh['seq'=4,'fsdp'=8] {'fsdp'}, dimensions={0}, use_global_device_ids=true | all-gather | bytes 4608 | tf_op jit(solution)/shard_map/all_gather | solution.py:137
  1154.3 39.8 %while.30 = (s32[]{:T(128)}, bf16[4,256,8,64]{1,3,2,0:T(8,128)(2,1)S(1)}, f32[4,8,256,1]{2,1,3,0:T(8,128)S(1)}, s32[4]{0:T(128)S(1)}, bf16[1024,32,64]{0,2,1:T(8...) while((s32[]{:T(128)}, ...), condition=%wide.region_5.6_spmd.clone.clone, body=%wide.region_2.5_spmd.clone.sunk.clone | while | flops 560199680 | bytes 29169844 | solution.py:133
  1202.0 13.8 fusion.78
  1215.8 14.1 fusion.79
  1229.9 28.0 multiply_convert_fusion.1
  1257.9 12.7 fusion.80
  1270.6 151.0 %all-gather.25.cloned.1.call-done = bf16[2048,5632]{1,0:T(8,128)(2,1)} async-done(((bf16[256,5632]{1,0:T(8,128)(2,1)}), bf16[2048,5632]{1,0:T(8,128)(2,1)}) %all-gather.25.cloned.1.call-update) | async-done | bytes 23068688 | tf_op jit(solution)/shard_map/all_gather | solution.py:162
  1421.6 13.8 multiply_reduce_fusion.1
  1445.6 80.3 %while.31 = (s32[]{:T(128)}, f32[4,256,8,64]{1,3,2,0:T(8,128)}, f32[4,1024,8,64]{1,3,2,0:T(8,128)}, f32[4,1024,8,64]{1,3,2,0:T(8,128)}, s32[4]{0:T(128)S(1)}, /*...) while((s32[]{:T(128)}, f32[4,256,8,64]{1,3,2,0:T(8,128)}, ...), condition=%wide.region_12.13_spmd.clone.clone, body=%wide.region_10.12_spmd.clone.sunk.clone | while | flops 1374550016 | bytes 72940760 | solution.py:235
  1549.6 60.9 %reduce-scatter.9.cloned.1.call-done = f32[256,2048]{0,1:T(8,128)} async-done(((f32[1024,2048]{0,1:T(8,128)}), f32[256,2048]{0,1:T(8,128)}) %reduce-scatter.9.cloned.1.call-update) | async-done | bytes 2097168 | tf_op jit(solution)/shard_map/reduce_scatter | solution.py:240
  1612.1 87.9 %reduce-scatter.11.cloned.1.call-done = f32[256,2048]{0,1:T(8,128)} async-done(((f32[1024,2048]{0,1:T(8,128)}), f32[256,2048]{0,1:T(8,128)}) %reduce-scatter.11.cloned.1.call-update) | async-done | bytes 2097168 | tf_op jit(solution)/shard_map/reduce_scatter | solution.py:241
  1705.0 15.0 convolution_convert_fusion.2
  1721.6 21.3 convolution_convert_fusion
  1743.0 48.7 %reduce-scatter.15.cloned.1.call-done = bf16[256,2048]{1,0:T(8,128)(2,1)} async-done(((bf16[2048,2048]{1,0:T(8,128)(2,1)}), bf16[256,2048]{1,0:T(8,128)(2,1)}) %reduce-scatter.15.cloned.1.call-update) | async-done | bytes 1048592 | tf_op jit(solution)/shard_map/reduce_scatter | solution.py:197
  1791.7 228.2 %reduce-scatter.17.cloned.1.call-done = bf16[704,2048]{1,0:T(8,128)(2,1)} async-done(((bf16[5632,2048]{1,0:T(8,128)(2,1)}), bf16[704,2048]{1,0:T(8,128)(2,1)}) %reduce-scatter.17.cloned.1.call-update) | async-done | bytes 2883600 | tf_op jit(solution)/shard_map/reduce_scatter | solution.py:189
  2019.9 247.8 %reduce-scatter.13.cloned.1.call-done = bf16[256,6144]{1,0:T(8,128)(2,1)} async-done(((bf16[2048,6144]{1,0:T(8,128)(2,1)}), bf16[256,6144]{1,0:T(8,128)(2,1)}) %reduce-scatter.13.cloned.1.call-update) | async-done | bytes 3145744 | tf_op jit(solution)/shard_map/reduce_scatter | solution.py:261
  2267.7 444.5 %reduce-scatter.19.cloned.1.call-done = bf16[256,11264]{1,0:T(8,128)(2,1)} async-done(((bf16[2048,11264]{1,0:T(8,128)(2,1)}), bf16[256,11264]{1,0:T(8,128)(2,1)}) %reduce-scatter.19.cloned.1.call-update) | async-done | bytes 5767184
  2714.8 13.8 fusion.53
  2729.6 14.0 fusion.61
  2743.6 26.0 all-reduce.6
  2787.0 171.4 %all-reduce.11.cloned.1.call-done = (bf16[256,6144]{1,0:T(8,128)(2,1)}, bf16[256,2048]{1,0:T(8,128)(2,1)}, bf16[256,11264]{1,0:T(8,128)(2,1)}, bf16[704,2048]{1,0:T(8,128)(2,1)}) async-done(((bf16[256,6144]{1,0:T(8,128)(2,1)}, bf16[256,2048]{1,0:T(8,128)(2,1)}, bf16[256,11264]{1,0:T(8,128)(2,1)}, bf16[704,2048]{1,0:T(8,128)(2,1)}), (bf16[256,6144]{1,0:T(8,128)(2,1)}, bf16[256,2048]{1,0:T(8,128)(2,1)}, ...) | async-done | bytes 12845072 | tf_op jit(solution)/shard_map/psum | solution.py:289
  (278 shorter events, 281.3 us)
Async XLA Ops:
  7.2 225.2 %all-gather.13.cloned.1.call-start = ((), (), s32[]{:S(2)}) async-start(), calls=%async_computation.7 | async-start | bytes 28311552 | tf_op jit(solution)/shard_map/all_gather | solution.py:87
  8.0 1139.7 %all-gather.15.cloned.1.call-start = ((), (), s32[]{:S(2)}) async-start(), calls=%async_computation.8 | async-start | bytes 5242880 | tf_op jit(solution)/shard_map/all_gather | solution.py:107
  35.9 208.3 %copy-start.26 = (f32[8,1,256]{2,1,0:T(1,128)}, f32[8,1,256]{2,1,0:T(1,128)S(1)}, u32[]{:S(2)}) copy-start(f32[8,1,256]{2,1,0:T(1,128)S(1)} %convert_element_type.193) | copy-start | bytes 24580
  47.7 196.5 %copy-start.22 = (f32[8,1,256]{2,1,0:T(1,128)}, f32[8,1,256]{2,1,0:T(1,128)S(1)}, u32[]{:S(2)}) copy-start(f32[8,1,256]{2,1,0:T(1,128)S(1)} %convert_element_type.192) | copy-start | bytes 24580
  47.9 196.3 %copy-start.34 = (f32[256]{0:T(256)}, f32[256]{0:T(256)S(1)}, u32[]{:S(2)}) copy-start(f32[256]{0:T(256)S(1)} %broadcast_multiply_fusion.7) | copy-start | bytes 3076
  248.1 906.2 %all-gather.17.cloned.1.call-start = ((), (), s32[]{:S(2)}) async-start(), calls=%async_computation.9 | async-start | bytes 5242880 | tf_op jit(solution)/shard_map/all_gather | solution.py:106
  262.0 932.2 %all-gather.19.cloned.1.call-start = ((), (), s32[]{:S(2)}) async-start(), calls=%async_computation.10 | async-start | bytes 9437184 | tf_op jit(solution)/shard_map/all_gather | solution.py:89
  262.6 953.2 %all-gather.21.cloned.1.call-start = ((), (), s32[]{:S(2)}) async-start(), calls=%async_computation.11 | async-start | bytes 25952256 | tf_op jit(solution)/shard_map/all_gather | solution.py:139
  263.2 966.7 %all-gather.23.cloned.1.call-start = ((), (), s32[]{:S(2)}) async-start(), calls=%async_computation.12 | async-start | bytes 25952256 | tf_op jit(solution)/shard_map/all_gather | solution.py:141
  272.8 604.3 %copy-start.48 = (bf16[256]{0:T(256)(128)(2,1)S(1)}, bf16[256]{0:T(256)(128)(2,1)}, u32[]{:S(2)}) copy-start(bf16[256]{0:T(256)(128)(2,1)} %param.25) | copy-start | bytes 1540
  272.8 929.2 %all-to-all-start = ((bf16[8,256,5632]{2,1,0:T(8,128)(2,1)}), bf16[8,256,5632]{2,1,0:T(8,128)(2,1)}, u32[]{:S(2)}, u32[]{:S(2)}) async-start(bf16[8,256,5632]{2,1,0:T(8,128)(2,1)} %stack.2), calls=%async_computation | async-start | bytes 46137344 | tf_op jit(solution)/shard_map/all_to_all | solution.py:15
  279.2 1142.4 %all-gather.25.cloned.1.call-start = ((), (), s32[]{:S(2)}) async-start(), calls=%async_computation.13 | async-start | bytes 25952256 | tf_op jit(solution)/shard_map/all_gather | solution.py:162
  280.0 1330.6 %reduce-scatter.9.cloned.1.call-start = ((), (), s32[]{:S(2)}) async-start(), calls=%async_computation.14 | async-start | bytes 10485760 | tf_op jit(solution)/shard_map/reduce_scatter | solution.py:240
  877.0 338.7 %copy-start.28 = (f32[8,1,256]{2,1,0:T(1,128)}, f32[8,1,256]{2,1,0:T(1,128)S(1)}, u32[]{:S(2)}) copy-start(f32[8,1,256]{2,1,0:T(1,128)S(1)} %convert_element_type.196) | copy-start | bytes 24580
  1145.8 289.6 %copy-start.24 = (f32[8,1,256]{2,1,0:T(1,128)}, f32[8,1,256]{2,1,0:T(1,128)S(1)}, u32[]{:S(2)}) copy-start(f32[8,1,256]{2,1,0:T(1,128)S(1)} %convert_element_type.195) | copy-start | bytes 24580
  1201.6 233.8 %copy-start = (f32[256,2048]{1,0:T(8,128)}, f32[256,2048]{1,0:T(8,128)S(1)}, u32[]{:S(2)}) copy-start(f32[256,2048]{1,0:T(8,128)S(1)} %get-tuple-element.285) | copy-start | bytes 6291460
  1201.6 233.8 %copy-start.30 = (f32[256]{0:T(256)}, f32[256]{0:T(256)S(1)}, u32[]{:S(2)}) copy-start(f32[256]{0:T(256)S(1)} %broadcast_multiply_fusion.6) | copy-start | bytes 3076
  1202.0 233.4 %copy-start.32 = (f32[256]{0:T(256)}, f32[256]{0:T(256)S(1)}, u32[]{:S(2)}) copy-start(f32[256]{0:T(256)S(1)} %add_rsqrt_fusion) | copy-start | bytes 3076
  1525.9 174.1 %reduce-scatter.11.cloned.1.call-start = ((), (), s32[]{:S(2)}) async-start(), calls=%async_computation.15 | async-start | bytes 10485760 | tf_op jit(solution)/shard_map/reduce_scatter | solution.py:241
  1526.7 265.0 %reduce-scatter.15.cloned.1.call-start = ((), (), s32[]{:S(2)}) async-start(), calls=%async_computation.17 | async-start | bytes 9437184 | tf_op jit(solution)/shard_map/reduce_scatter | solution.py:197
  1533.5 486.4 %reduce-scatter.17.cloned.1.call-start = ((), (), s32[]{:S(2)}) async-start(), calls=%async_computation.18 | async-start | bytes 25952256 | tf_op jit(solution)/shard_map/reduce_scatter | solution.py:189
  1547.9 719.8 %reduce-scatter.13.cloned.1.call-start = ((), (), s32[]{:S(2)}) async-start(), calls=%async_computation.16 | async-start | bytes 28311552 | tf_op jit(solution)/shard_map/reduce_scatter | solution.py:261
  1720.0 992.2 %reduce-scatter.19.cloned.1.call-start = ((), (), s32[]{:S(2)}) async-start(), calls=%async_computation.19 | async-start | bytes 51904512
  1742.9 1215.4 %all-reduce.11.cloned.1.call-start = ((), (), s32[]{:S(2)}) async-start(), calls=%async_computation.20 | async-start | bytes 25690112 | tf_op jit(solution)/shard_map/psum | solution.py:289
  (43 other events, 819.1 us)
Sparse Core Ops, SparseCore 0:
  9.7 222.6 all-gather.12
  248.2 50.6 all-gather.14
  301.3 52.4 all-gather.16
  355.3 167.6 all-gather.18
  524.5 463.9 all-gather.20
  990.0 228.3 all-gather.22
  1220.0 201.5 all-gather.24
  1526.0 84.4 reduce-scatter.8
  1613.6 86.2 reduce-scatter.10
  1702.1 89.5 reduce-scatter.14
  1794.0 225.7 reduce-scatter.16
  2022.1 245.5 reduce-scatter.12
  2270.1 442.0 reduce-scatter.18
  2716.0 242.3 all-reduce.10
